TPU v7x, 32 devices: a whole 2x2x4 slice. The times are simulated.
32 devices in a mesh: replica: 8 (over z, core), ctx: 4 (over y, x).
Axes of the slice: x: 2, y: 2, z: 4, core: 2. Of those that a mesh axis runs over, the one named last changes fastest.
Arguments:
- queries: bfloat16 [32, 128, 3584], P('replica', 'ctx'), may hold values from -128 to 128
- key_cache: bfloat16 [4096, 512], P('ctx'), may hold values from -6 to 6
- value_cache: bfloat16 [4096, 512], P('ctx'), may hold values from -6 to 6
- key_scale: float32 [32, 4], P('ctx'), may hold values from 0.7 to 1.4
- value_scale: float32 [32, 4], P('ctx'), may hold values from 0.5 to 2
- pattern: int32 [28, 32, 32], replicated, may hold values from 0 to 31
- target: int32 [32], replicated, may hold values from 0 to 7, as said below
Outputs:
- landed: bfloat16 [32, 128, 3584], P('replica', 'ctx')
Inputs may be any that keep to these rules, and one draw needn't show every extreme that they name: `target`: query block j belongs to group j // 4. The blocks of one group go to distinct groups, and every group receives exactly 4 blocks.
All inputs are finite; a program needn't handle non-finite values.
Results may differ from a plain program's by a relative error of at most 0.018.
Values may be sent and summed in bfloat16 or wider, within the bound.
No kernel may reach another device: no remote copies, remote signals or barrier semaphores. Data moves between devices by JAX's collectives and lax.ppermute only.
A program may use at most 64 MiB of HBM per device.

v0:
```python
import math

import jax
import jax.numpy as jnp
from jax import lax
from jax.sharding import PartitionSpec as P


def arrivals(target, group_index, group_count, per_group):
    block_grid = target.reshape(group_count, per_group)
    hit_table = (block_grid == group_index).astype(jnp.int32)
    coming = jnp.sum(hit_table, axis=1)
    arrival_slot = jnp.cumsum(coming) - 1
    places = jnp.arange(per_group, dtype=jnp.int32)
    matched = (coming[None, :] > 0) & (arrival_slot[None, :] == places[:, None])
    anchor = jnp.arange(group_count, dtype=jnp.int32) * per_group + jnp.sum(
        hit_table * places[None, :], axis=1
    )
    arriving = jnp.sum(jnp.where(matched, anchor[None, :], 0), axis=1)
    return (matched.astype(jnp.bfloat16), arriving)


def relocate(blocks, target, group_index, group_count, per_group, picker):
    own_targets = lax.dynamic_slice_in_dim(target, group_index * per_group, per_group)
    outgoing = (own_targets[None, :] == jnp.arange(group_count, dtype=jnp.int32)[:, None]).astype(
        jnp.bfloat16
    )
    packed = jnp.einsum("dk,kxh->dxh", outgoing, blocks, preferred_element_type=jnp.float32).astype(
        jnp.bfloat16
    )
    received = lax.all_to_all(packed, "replica", split_axis=0, concat_axis=0, tiled=True)
    return jnp.einsum("sr,rxh->sxh", picker, received, preferred_element_type=jnp.float32).astype(
        jnp.bfloat16
    )


def collect(blocks):
    return lax.all_gather(blocks, "ctx", axis=1, tiled=True)


def attend(
    whole,
    block_list,
    key_cache,
    value_cache,
    key_scale,
    value_scale,
    pattern,
    shard_index,
    kv_blocks,
):
    block_count, block_rows, row_width = whole.shape
    kv_heads = key_scale.shape[1]
    head_size = key_cache.shape[1] // kv_heads
    head_count = row_width // head_size
    group_size = head_count // kv_heads
    local_blocks = key_cache.shape[0] // block_rows
    first_block = kv_blocks - pattern.shape[1]
    query = whole.reshape(block_count, block_rows, kv_heads, group_size, head_size)
    keys = key_cache.reshape(local_blocks, block_rows, kv_heads, head_size)
    values = value_cache.reshape(local_blocks, block_rows, kv_heads, head_size)
    listed = jnp.take(pattern, block_list, axis=1).reshape(
        kv_heads, group_size, block_count, pattern.shape[2]
    )
    diagonal = first_block + block_list
    row_ids = jnp.arange(block_rows, dtype=jnp.int32)
    block_ids = shard_index * local_blocks + jnp.arange(local_blocks, dtype=jnp.int32)
    key_pos = block_ids[:, None] * block_rows + row_ids[None, :]
    inv_root = 1.0 / math.sqrt(head_size)

    def one_item(item):
        block_slot = item // kv_heads
        head = item % kv_heads
        query_tile = lax.dynamic_index_in_dim(
            lax.dynamic_index_in_dim(query, block_slot, 0, keepdims=False), head, 1, keepdims=False
        )
        key_head = lax.dynamic_index_in_dim(keys, head, 2, keepdims=False)
        value_head = lax.dynamic_index_in_dim(values, head, 2, keepdims=False)
        heads_listed = lax.dynamic_index_in_dim(
            lax.dynamic_index_in_dim(listed, head, 0, keepdims=False), block_slot, 1, keepdims=False
        )
        diag = lax.dynamic_index_in_dim(diagonal, block_slot, 0, keepdims=False)
        chosen = (
            jnp.any(heads_listed[:, :, None] == block_ids[None, None, :], axis=1)
            | (block_ids == diag)[None, :]
        )
        query_pos = diag * block_rows + row_ids
        causal = key_pos[None, :, :] <= query_pos[:, None, None]
        allowed = chosen[:, None, :, None] & causal[None]
        key_factor = lax.dynamic_index_in_dim(key_scale, head, 1, keepdims=False) * inv_root
        value_factor = lax.dynamic_index_in_dim(value_scale, head, 1, keepdims=False)
        product = jnp.einsum(
            "rkd,btd->krbt", query_tile, key_head, preferred_element_type=jnp.float32
        )
        scores = product * key_factor[None, None, :, None]
        local_top = jnp.max(jnp.where(allowed, scores, -jnp.inf), axis=(2, 3))
        expo = jnp.where(allowed, jnp.exp(scores - local_top[:, :, None, None]), 0.0)
        weight = (expo * value_factor[None, None, :, None]).astype(jnp.bfloat16)
        numer = jnp.einsum("krbt,btd->rkd", weight, value_head, preferred_element_type=jnp.float32)
        denom = jnp.transpose(jnp.sum(expo, axis=(2, 3)))
        return (numer, denom, jnp.transpose(local_top))

    numer_all, denom_all, top_all = lax.map(
        one_item, jnp.arange(block_count * kv_heads, dtype=jnp.int32)
    )
    numer_all = numer_all.reshape(block_count, kv_heads, block_rows, group_size, head_size)
    denom_all = denom_all.reshape(block_count, kv_heads, block_rows, group_size)
    local_top = top_all.reshape(block_count, kv_heads, block_rows, group_size)
    top_score = lax.pmax(local_top.astype(jnp.bfloat16), "ctx").astype(local_top.dtype)
    rescale = jnp.exp(local_top - top_score)
    numer_scaled = jnp.transpose(numer_all * rescale[..., None], (0, 2, 1, 3, 4)).reshape(
        block_count, block_rows, row_width
    )
    denom_scaled = jnp.transpose(denom_all * rescale, (0, 2, 1, 3)).reshape(
        block_count, block_rows, head_count
    )
    numer_sum, denom_sum = (
        lax.psum_scatter(
            numer_scaled.astype(jnp.bfloat16), "ctx", scatter_dimension=1, tiled=True
        ).astype(jnp.float32),
        lax.psum_scatter(
            denom_scaled.astype(jnp.bfloat16), "ctx", scatter_dimension=1, tiled=True
        ).astype(jnp.float32),
    )
    own_rows = numer_sum.shape[1]
    attended = (
        numer_sum.reshape(block_count, own_rows, head_count, head_size) / denom_sum[..., None]
    )
    return attended.reshape(block_count, own_rows, row_width).astype(jnp.bfloat16)


def per_device(queries, key_cache, value_cache, key_scale, value_scale, pattern, target):
    group_count = lax.axis_size("replica")
    shard_count = lax.axis_size("ctx")
    group_index = lax.axis_index("replica")
    shard_index = lax.axis_index("ctx")
    per_group = queries.shape[0]
    block_rows = queries.shape[1] * shard_count
    kv_blocks = key_cache.shape[0] // block_rows * shard_count
    picker, arriving = arrivals(target, group_index, group_count, per_group)
    moved = relocate(queries, target, group_index, group_count, per_group, picker)
    whole = collect(moved)
    return attend(
        whole,
        arriving,
        key_cache,
        value_cache,
        key_scale,
        value_scale,
        pattern,
        shard_index,
        kv_blocks,
    )


def solution(mesh):
    return jax.shard_map(
        per_device,
        mesh=mesh,
        in_specs=(
            P("replica", "ctx", None),
            P("ctx", None),
            P("ctx", None),
            P("ctx", None),
            P("ctx", None),
            P(),
            P(),
        ),
        out_specs=P("replica", "ctx", None),
        check_vma=False,
    )
```

profile of v0, /device:TPU:0, one launch (start us, length us, event | category | flops | bytes accessed | tf_op | source)
XLA Modules:
  0.0 480.7 jit_solution(8024060534990406194)
XLA Ops:
  8.8 1.8 copy.52
  10.5 6.4 %all-to-all-start = ((bf16[8,32,3584]{2,1,0:T(8,128)(2,1)}), bf16[8,32,3584]{2,1,0:T(8,128)(2,1)S(1)}, u32[]{:S(2)}, u32[]{:S(2)}) async-start(bf16[8,32,3584]{2,1,0:T(8,128)(2,1)} %copy.52), calls=%async_computation | async-start | bytes 3670016 | tf_op jit(solution)/shard_map/all_to_all | solution.py:31
  17.4 42.9 %all-to-all-done = bf16[8,32,3584]{2,1,0:T(8,128)(2,1)S(1)} async-done(((bf16[8,32,3584]{2,1,0:T(8,128)(2,1)}), bf16[8,32,3584]{2,1,0:T(8,128)(2,1)S(1)}, u32[]{:S(2)}, u32[]{:S(2)}) %all-to-all-start) | async-done | bytes 1835040 | tf_op jit(solution)/shard_map/all_to_all | solution.py:31
  60.3 2.9 convolution_convert_fusion.1
  63.4 1.4 reshape.163
  64.8 1.5 copy.55
  67.8 42.8 %all-gather.2.cloned.1.call-done = bf16[4,128,3584]{2,0,1:T(4,128)(2,1)} async-done(((bf16[4,32,3584]{2,0,1:T(4,128)(2,1)}), bf16[4,128,3584]{2,0,1:T(4,128)(2,1)}) %all-gather.2.cloned.1.call-update) | async-done | bytes 3670032 | tf_op jit(solution)/shard_map/all_gather | solution.py:38
  110.6 7.2 %copy.54 = bf16[4,128,3584]{1,2,0:T(8,128)(2,1)} copy(bf16[4,128,3584]{2,0,1:T(4,128)(2,1)} %all-gather.2.cloned.1.call-done) | data formatting | bytes 7340032 | tf_op jit(solution)/shard_map/all_gather | solution.py:38
  117.8 209.7 %while.18 = (s32[]{:T(128)}, f32[16,128,7,128]{1,3,2,0:T(8,128)}, f32[16,128,7]{1,2,0:T(8,128)S(1)}, f32[16,128,7]{1,2,0:T(8,128)S(1)}, s32[16]{0:T(128)S(1)}, /...) while((s32[]{:T(128)}, f32[16,128,7,128]{1,3,2,0:T(8,128)}, ...), condition=%wide.region_8.9_spmd.clone, body=%wide.region_4.8_spmd.clone.sunk | while | flops 483658688 | bytes 12792716 | solution.py:103
  124.3 1.7 fusion.45
  126.1 1.1 fusion.48
  127.8 3.1 fusion.47
  137.4 1.7 fusion.45
  139.1 1.1 fusion.48
  140.9 3.1 fusion.47
  150.5 1.7 fusion.45
  152.3 1.1 fusion.48
  154.1 3.1 fusion.47
  163.6 1.7 fusion.45
  165.4 1.1 fusion.48
  167.2 3.1 fusion.47
  176.8 1.7 fusion.45
  178.5 1.1 fusion.48
  180.3 3.1 fusion.47
  189.9 1.7 fusion.45
  191.6 1.1 fusion.48
  193.4 3.1 fusion.47
  203.0 1.7 fusion.45
  204.7 1.1 fusion.48
  206.5 3.1 fusion.47
  216.1 1.7 fusion.45
  217.8 1.1 fusion.48
  219.6 3.0 fusion.47
  229.2 1.7 fusion.45
  230.9 1.1 fusion.48
  232.7 3.1 fusion.47
  242.3 1.7 fusion.45
  245.8 3.1 fusion.47
  255.4 1.7 fusion.45
  258.9 3.0 fusion.47
  268.5 1.7 fusion.45
  272.0 3.1 fusion.47
  281.6 1.7 fusion.45
  283.3 1.1 fusion.48
  285.1 3.1 fusion.47
  294.7 1.7 fusion.45
  296.4 1.1 fusion.48
  298.2 3.0 fusion.47
  307.8 1.7 fusion.45
  309.5 1.1 fusion.48
  311.3 3.1 fusion.47
  320.9 1.7 fusion.45
  324.4 3.1 fusion.47
  327.5 15.4 %pmax.7 = bf16[4,4,128,7]{2,0,3,1:T(4,128)(2,1)S(1)} all-reduce(bf16[4,4,128,7]{2,0,3,1:T(4,128)(2,1)S(1)} %copy.87), channel_id=1, replica_groups=mesh['replica'=8,'ctx'=4] {'ctx'}, use_global_device_ids=true, to_apply=%region_9.10 | all-reduce | flops 14336 | bytes 57344 | tf_op jit(solution)/shard_map/pmax | solution.py:109
  343.1 1.5 copy.73
  344.6 2.3 reshape.165
  347.0 6.2 %multiply_convert_fusion.6 = bf16[4,4,128,7,128]{2,4,3,1,0:T(8,128)(2,1)} fusion(f32[4,4,128,7,128]{2,4,3,1,0:T(8,128)} %bitcast.9, f32[4,4,128,7]{2,3,1,0:T(8,128)S(1)} %copy.60), kind=kLoop, calls=%fused_computation.39 | loop fusion | flops 3670016 | bytes 11067392 | tf_op jit(solution)/shard_map/convert_element_type | solution.py:119
  353.3 7.3 %copy.61 = bf16[4,128,3584]{2,0,1:T(4,128)(2,1)} copy(bf16[4,128,3584]{1,2,0:T(8,128)(2,1)} %bitcast.121) | data formatting | bytes 7340032 | tf_op jit(solution)/shard_map/convert_element_type | solution.py:119
  362.6 8.6 %reduce-scatter.4.cloned.1.call-done = bf16[32,112]{1,0:T(8,128)(2,1)} async-done(((bf16[128,112]{1,0:T(8,128)(2,1)}), bf16[32,112]{1,0:T(8,128)(2,1)}) %reduce-scatter.4.cloned.1.call-update) | async-done | bytes 7184
  371.1 1.2 reshape.166
  373.4 1.6 div.20
  375.1 94.9 %all-reduce.3.cloned.1.call-done = bf16[4,128,3584]{2,0,1:T(4,128)(2,1)} async-done(((bf16[4,128,3584]{2,0,1:T(4,128)(2,1)}), bf16[4,128,3584]{2,0,1:T(4,128)(2,1)}) %all-reduce.3.cloned.1.call-update) | async-done | bytes 3670032
  469.9 1.5 constant_dynamic-slice_fusion.2
  471.4 2.7 divide_convert_fusion
  (275 shorter events, 73.5 us)
Async XLA Ops:
  6.5 1.2 copy-start
  8.7 8.2 %copy-start.4 = (s32[32]{0:T(128)S(1)}, s32[32]{0:T(128)}, u32[]{:S(2)}) copy-start(s32[32]{0:T(128)} %param.15) | copy-start | bytes 388
  10.5 49.8 %all-to-all-start = ((bf16[8,32,3584]{2,1,0:T(8,128)(2,1)}), bf16[8,32,3584]{2,1,0:T(8,128)(2,1)S(1)}, u32[]{:S(2)}, u32[]{:S(2)}) async-start(bf16[8,32,3584]{2,1,0:T(8,128)(2,1)} %copy.52), calls=%async_computation | async-start | bytes 3670016 | tf_op jit(solution)/shard_map/all_to_all | solution.py:31
  16.9 93.7 %all-gather.2.cloned.1.call-start = ((), (), s32[]{:S(2)}) async-start(), calls=%async_computation.2 | async-start | bytes 4587520 | tf_op jit(solution)/shard_map/all_gather | solution.py:38
  63.2 3.0 copy-start.1
  63.3 307.9 %reduce-scatter.4.cloned.1.call-start = ((), (), s32[]{:S(2)}) async-start(), calls=%async_computation.3 | async-start | bytes 40960
  64.8 2.1 copy-start.2
  67.7 50.1 %copy-start.3 = (f32[16,128,7]{1,2,0:T(8,128)S(1)}, f32[16,128,7]{1,2,0:T(8,128)}, u32[]{:S(2)}) copy-start(f32[16,128,7]{1,2,0:T(8,128)} %custom-call.3) | copy-start | bytes 172036
  347.0 123.0 %all-reduce.3.cloned.1.call-start = ((), (), s32[]{:S(2)}) async-start(), calls=%async_computation.4 | async-start | bytes 7340032
  360.6 0.7 copy-start.5
Sparse Core Ops, SparseCore 0:
  63.4 47.1 all-gather.1
  347.1 23.9 reduce-scatter.3
  374.2 95.6 all-reduce.2
where the time goes:
time: 484 us; the launch traced here: 481 us
  waiting for transfers between devices  189 us (39%)
  matrix products  80.3 us (17%)
  local copies, waits for them, and re-layouts  63.9 us (13%)
  other arithmetic  57.7 us (12%)
  loops' own time  53.7 us (11%)
  blocking collectives  15.4 us (3%)
  between operations  14 us (3%)
  starting transfers between devices  6.47 us (1%)
    unnamed x5, waiting for transfers between devices  104 us
    another operation x1, loops' own time, attend(): lax.map(one_item, jnp.arange(block_count * kv_heads, dtype=jnp.int32))  53.7 us
    dot_general x16, matrix products, one_item(): jnp.einsum('krbt,btd->rkd', weight, value_head, preferred_element_type=jn...  49 us
    all_to_all x1, waiting for transfers between devices, relocate(): lax.all_to_all(packed, 'replica', split_axis=0, concat_axis=0, tiled=True)  42.9 us
    all_gather x1, waiting for transfers between devices, collect(): return lax.all_gather(blocks, 'ctx', axis=1, tiled=True)  42.8 us
    dot_general x16, matrix products, one_item(): jnp.einsum('rkd,btd->krbt', query_tile, key_head, preferred_element_type=...  27.4 us
    reduce_sum x16, other arithmetic, one_item(): denom = jnp.transpose(jnp.sum(expo, axis=(2, 3)))  17.3 us
    pmax x1, blocking collectives, attend(): lax.pmax(local_top.astype(jnp.bfloat16), 'ctx').astype(local_top.dtype)  15.4 us
  transfers between devices with their start and end apart: 4, of which 4 were waited for; matrix products, arithmetic and copies ran while one was open for 5% of the time, Pallas kernels for 0%

commit v1 on v0

v1 whole, which is shorter than its diff:
```python
import functools
import math

import jax
import jax.numpy as jnp
from jax import lax
from jax.experimental import pallas as pl
from jax.experimental.pallas import tpu as pltpu
from jax.sharding import PartitionSpec as P


MASKED = -1e30
SIZES = (8, 4, 2)
NT = (((1,), (1,)), ((), ()))
VMEM = pl.BlockSpec(memory_space=pltpu.VMEM)
SMEM = pl.BlockSpec(memory_space=pltpu.SMEM)


class Plan:
    def __init__(self, queries, key_cache, key_scale, pattern, groups, shards):
        self.groups, self.shards = groups, shards
        self.per_group, self.chunk, self.row_width = queries.shape
        self.rows = self.chunk * shards
        self.kv_heads = key_scale.shape[1]
        self.width = key_cache.shape[1] // self.kv_heads
        self.group = self.row_width // self.width // self.kv_heads
        self.span = self.group * self.width
        self.local_blocks = key_scale.shape[0]
        self.local_rows = key_cache.shape[0]
        self.kv_blocks = self.local_blocks * shards
        self.kv_rows = self.local_rows * shards
        self.first_block = self.kv_blocks - pattern.shape[1]
        self.repeat = shards // self.kv_heads
        self.slots = self.per_group // self.repeat
        self.scale_rows = -(-3 * self.local_blocks // 16) * 16
        self.sourced = self.group * 3 // 7
        self.landed = self.group - self.sourced
        self.stride = max(self.chunk, 16)
        self.near_rows = self.sourced * self.slots * self.stride

    def cache_rows(self, relative):
        count = 2 * self.local_rows if relative == 0 else self.local_rows
        return count + self.scale_rows


def aligned(index, size):
    return pl.ds(pl.multiple_of(index * size, size), size)


def pack_far(plan, target, q_ref, far):
    group = lax.axis_index("replica")
    wide = plan.sourced * plan.width
    for d in range(plan.shards):
        head = d // plan.repeat
        for k in range(plan.per_group):
            far[target[group * plan.per_group + k], d] = q_ref[
                k, :, pl.ds(head * plan.span + wide, plan.landed * plan.width)
            ]


def pack_near(plan, ks_ref, vs_ref, k_ref, v_ref, q_ref, *refs):
    outs, factors = refs[: plan.shards], refs[plan.shards]
    group, me = lax.axis_index("replica"), lax.axis_index("ctx")
    rows, width, blocks = plan.rows, plan.width, plan.local_blocks
    half = group % 2
    lane = lax.broadcasted_iota(jnp.int32, ks_ref.shape, 1)
    for c in range(plan.shards):
        at = me ^ c
        head, part = at // plan.repeat, at % plan.repeat
        lanes = aligned(head, width)

        def column(ref):
            picked = jnp.sum(jnp.where(lane == head, ref[...], 0.0), axis=1, keepdims=True)
            return jnp.broadcast_to(picked, (blocks, width))

        factors[...] = column(vs_ref)
        count = blocks if c == 0 else blocks // 2
        first = 0 if c == 0 else half * count
        out = outs[c]
        for i in range(count):
            b = first + i
            out[pl.ds(i * rows, rows), :] = k_ref[aligned(b, rows), lanes]
            out[pl.ds((count + i) * rows, rows), :] = (
                v_ref[aligned(b, rows), lanes].astype(jnp.float32) * factors[pl.ds(b, 1), :]
            ).astype(jnp.bfloat16)
        x = column(ks_ref)
        high = x.astype(jnp.bfloat16).astype(jnp.float32)
        middle = (x - high).astype(jnp.bfloat16).astype(jnp.float32)
        low = x - high - middle
        spare = plan.scale_rows - 3 * blocks
        terms = [high, middle, low]
        if spare:
            terms.append(jnp.zeros((spare, width), jnp.float32))
        out[pl.ds(2 * count * rows, plan.scale_rows), :] = jnp.concatenate(terms, axis=0).astype(
            jnp.bfloat16
        )
        base = plan.cache_rows(c)
        for r in range(plan.sourced):
            for k in range(plan.slots):
                out[pl.ds(base + (r * plan.slots + k) * plan.stride, plan.chunk), :] = q_ref[
                    part * plan.slots + k,
                    :,
                    pl.ds(pl.multiple_of(head * plan.span + r * width, width), width),
                ]


def attend_body(plan, far, step, *refs):
    n = plan.shards
    target, refs = refs[0], refs[1:]
    if far:
        received, keys, values, scale, pattern = refs[:5]
        outs, refs = refs[5 : 5 + n], refs[5 + n :]
    else:
        own, direct, swapped = refs[0], refs[1:n], refs[n : 2 * n - 1]
        pattern, out, keys, values, scale = refs[2 * n - 1 : 2 * n + 4]
        refs = refs[2 * n + 4 :]
    q_aug, bias_rows, score, top, acc, loose, blocks = refs

    group, me = lax.axis_index("replica"), lax.axis_index("ctx")
    rows, width, slots = plan.rows, plan.width, plan.slots
    head_count = plan.landed if far else plan.sourced
    head_first = plan.sourced if far else 0
    my_head, my_part = me // plan.repeat, me % plan.repeat
    half = group % 2

    def take(ref, count, block):
        size = count * rows
        at = pl.ds(pl.multiple_of(block * rows, rows), size)
        keys[at, :] = ref[pl.ds(0, size), :]
        values[at, :] = ref[pl.ds(size, size), :]

    if not far:
        size = plan.local_blocks
        some = size // 2
        factor = 1.0 / (math.sqrt(width) * math.log(2.0))
        for c in range(n):
            shard = me ^ c
            if c == 0:
                take(own, size, shard * size)
            else:
                take(direct[c - 1], some, shard * size + half * some)
                take(swapped[c - 1], some, shard * size + (1 - half) * some)
            tail = (own if c == 0 else direct[c - 1])[
                pl.ds(plan.cache_rows(c) - plan.scale_rows, plan.scale_rows), :
            ].astype(jnp.float32)
            scale[aligned(shard, size), :] = (
                tail[:size] + tail[size : 2 * size] + tail[2 * size : 3 * size]
            ) * factor

    if far:

        def scan(j, found):
            hit = target[j] == group

            @pl.when(hit)
            def _():
                blocks[found] = j

            return found + hit.astype(jnp.int32)

        lax.fori_loop(0, target.shape[0], scan, 0)

    lane = lax.broadcasted_iota(jnp.int32, (rows, width), 1)
    causal = lane <= lax.broadcasted_iota(jnp.int32, (rows, width), 0)
    for r in range(step):
        q_aug[pl.ds(r * rows, rows), pl.ds(width, width)] = (lane == r).astype(jnp.bfloat16)
    kv_lane = lax.broadcasted_iota(jnp.int32, (plan.kv_blocks, width), 1)
    selected = pattern.shape[2]
    kv_id = lax.broadcasted_iota(jnp.int32, (plan.kv_blocks, selected), 0)
    kv_row = lax.broadcasted_iota(jnp.int32, (plan.kv_blocks, width), 0)
    hold = score.shape[1] - width

    def one(k, head_from):
        block = blocks[my_part * slots + k] if far else (
            group * plan.per_group + my_part * slots + k
        )
        diag = plan.first_block + block
        bias = jnp.full((plan.kv_blocks, width), MASKED, jnp.float32)
        for r in range(step):
            listed = pattern[
                my_head * plan.group + head_first + head_from + r, pl.ds(block, 1), :
            ]
            hit = jnp.max(
                jnp.where(kv_id == listed, 1.0, 0.0), axis=1, keepdims=True
            )
            bias = jnp.where((kv_lane == r) & (hit > 0.0) & (kv_row < diag), 0.0, bias)
        for b in range(plan.kv_blocks):
            bias_rows[pl.ds(b * rows, rows), :] = jnp.broadcast_to(
                bias[b : b + 1, :], (rows, width)
            ).astype(jnp.bfloat16)

        exact = plan.chunk % 16 == 0
        for r in range(step):
            span = pl.ds(r * rows, rows)
            cols = pl.ds((head_from + r) * width, width)
            if far:
                piece = received[block // plan.per_group, :, :, cols]
                if not exact:
                    piece = piece.astype(jnp.float32)
                q_aug[span, pl.ds(0, width)] = piece.reshape(rows, width).astype(jnp.bfloat16)
            else:
                for c in range(n):
                    piece = (own if c == 0 else direct[c - 1])[
                        pl.ds(
                            pl.multiple_of(
                                plan.cache_rows(c)
                                + ((head_from + r) * slots + k) * plan.stride,
                                16,
                            ),
                            plan.chunk,
                        ),
                        :,
                    ]
                    if exact:
                        q_aug[
                            pl.ds(
                                pl.multiple_of(r * rows + (me ^ c) * plan.chunk, plan.chunk),
                                plan.chunk,
                            ),
                            pl.ds(0, width),
                        ] = piece
                    else:
                        loose[aligned(me ^ c, plan.chunk), :] = piece.astype(jnp.float32)
                if not exact:
                    q_aug[span, pl.ds(0, width)] = loose[...].astype(jnp.bfloat16)

        end = pl.multiple_of(diag * rows, rows)
        own_key = keys[pl.ds(end, rows), :]
        own_scale = scale[pl.ds(diag, 1), :]
        for r in range(step):
            span = pl.ds(r * rows, rows)
            s = lax.dot_general(
                q_aug[span, pl.ds(0, width)], own_key, NT, preferred_element_type=jnp.float32
            )
            s = jnp.where(causal, s * own_scale, MASKED)
            score[span, pl.ds(hold, width)] = s
            top[span, :] = s

        def find(size, first):
            def body(i, carry):
                start = first + i * size
                at = pl.multiple_of(start * rows, rows)
                span = pl.ds(at, size * rows)
                key = jnp.concatenate([keys[span, :], bias_rows[span, :]], axis=1)
                whole = lax.dot_general(q_aug[...], key, NT, preferred_element_type=jnp.float32)
                for r in range(step):
                    span = pl.ds(r * rows, rows)
                    best = top[span, :]
                    for m in range(size):
                        s = (
                            whole[r * rows : (r + 1) * rows, m * rows : (m + 1) * rows]
                            * scale[pl.ds(start + m, 1), :]
                        )
                        score[span, pl.ds(pl.multiple_of(at + m * rows, rows), width)] = s
                        best = jnp.maximum(best, s)
                    top[span, :] = best
                return carry

            return body

        def sweep(make):
            done = 0
            for size in SIZES:
                left = diag - done
                count = left // size if size > 2 else (left + 1) // 2
                lax.fori_loop(0, count, make(size, done), 0)
                done = done + count * size

        sweep(find)

        def summed(at, size):
            return jnp.concatenate(
                [values[pl.ds(at, size), :], jnp.ones((size, width), jnp.bfloat16)], axis=1
            )

        own_value = summed(end, rows)
        for r in range(step):
            span = pl.ds(r * rows, rows)
            m = jnp.broadcast_to(jnp.max(top[span, :], axis=1, keepdims=True), (rows, width))
            top[span, :] = m
            p = jnp.exp2(score[span, pl.ds(hold, width)] - m).astype(jnp.bfloat16)
            acc[span, :] = jnp.dot(p, own_value, preferred_element_type=jnp.float32)

        def gather(size, first):
            def body(i, carry):
                at = pl.multiple_of((first + i * size) * rows, rows)
                value = summed(at, size * rows)
                for r in range(step):
                    span = pl.ds(r * rows, rows)
                    m = jnp.concatenate([top[span, :]] * size, axis=1)
                    p = jnp.exp2(score[span, pl.ds(at, size * width)] - m).astype(jnp.bfloat16)
                    acc[span, :] += jnp.dot(p, value, preferred_element_type=jnp.float32)
                return carry

            return body

        sweep(gather)

        for r in range(step):
            cols = pl.ds((head_from + r) * width, width)
            if far:
                for c in range(n):
                    span = pl.ds(
                        pl.multiple_of(r * rows + (me ^ c) * plan.chunk, plan.chunk), plan.chunk
                    )
                    outs[c][k, :, cols] = (
                        acc[span, pl.ds(0, width)] / acc[span, pl.ds(width, width)]
                    ).astype(jnp.bfloat16)
            else:
                span = pl.ds(r * rows, rows)
                res = acc[span, pl.ds(0, width)] / acc[span, pl.ds(width, width)]
                if exact:
                    res = res.astype(jnp.bfloat16)
                out[target[block], :, :, cols] = res.reshape(n, plan.chunk, width).astype(
                    jnp.bfloat16
                )

    def slot(k, carry):
        for head_from in range(0, head_count, step):
            one(k, head_from)
        return carry

    lax.fori_loop(0, slots, slot, 0)


def attend(plan, far, target, operands):
    heads = plan.landed if far else plan.sourced
    step = heads
    while step > 1 and (
        heads % step or step * plan.rows * (plan.kv_rows + plan.width) * 4 > 18 * 2**20
    ):
        step -= 1
    n = plan.shards
    bf16, f32 = jnp.bfloat16, jnp.float32
    if far:
        shape = [
            jax.ShapeDtypeStruct((plan.slots, plan.chunk, heads * plan.width), bf16)
            for _ in range(n)
        ]
    else:
        table = jax.ShapeDtypeStruct((plan.kv_rows, plan.width), bf16)
        shape = [
            jax.ShapeDtypeStruct((plan.groups, n, plan.chunk, heads * plan.width), bf16),
            table,
            table,
            jax.ShapeDtypeStruct((plan.kv_blocks, plan.width), f32),
        ]
    work = plan.slots * heads * plan.rows * plan.kv_rows * plan.width
    held = (
        sum(x.size * x.dtype.itemsize for x in [*operands, *shape])
        + 2 * plan.kv_rows * plan.width
        + step * plan.rows * (plan.kv_rows + 6 * plan.width) * 4
    )
    return pl.pallas_call(
        functools.partial(attend_body, plan, far, step),
        in_specs=[SMEM] + [VMEM] * len(operands),
        out_specs=[VMEM] * len(shape),
        out_shape=shape,
        scratch_shapes=[
            pltpu.VMEM((step * plan.rows, 2 * plan.width), bf16),
            pltpu.VMEM((plan.kv_rows, plan.width), bf16),
            pltpu.VMEM((step * plan.rows, plan.kv_rows + plan.width), f32),
            pltpu.VMEM((step * plan.rows, plan.width), f32),
            pltpu.VMEM((step * plan.rows, 2 * plan.width), f32),
            pltpu.VMEM((plan.rows, plan.width), f32),
            pltpu.SMEM((plan.per_group,), jnp.int32),
        ],
        compiler_params=pltpu.CompilerParams(
            vmem_limit_bytes=min(held + 6 * 2**20, 62 * 2**20)
        ),
        cost_estimate=pl.CostEstimate(
            flops=2 * work, bytes_accessed=8 * 2**20, transcendentals=work // plan.width // 2
        ),
        name="attend_far" if far else "attend_near",
    )(target, *operands)


def place_rows(plan, target, received, *refs):
    parts, out, blocks = refs[: plan.shards], refs[plan.shards], refs[plan.shards + 1]
    group, me = lax.axis_index("replica"), lax.axis_index("ctx")

    def scan(j, found):
        hit = target[j] == group

        @pl.when(hit)
        def _():
            blocks[found] = j

        return found + hit.astype(jnp.int32)

    lax.fori_loop(0, target.shape[0], scan, 0)
    wide = plan.sourced * plan.width
    for k in range(plan.per_group):
        source = blocks[k] // plan.per_group
        part = blocks[k] % plan.per_group // plan.slots
        for h in range(plan.kv_heads):
            out[k, :, pl.ds(h * plan.span, wide)] = received[source, h * plan.repeat + part]
    for c in range(plan.shards):
        at = me ^ c
        head, part = at // plan.repeat, at % plan.repeat
        out[
            pl.ds(part * plan.slots, plan.slots),
            :,
            pl.ds(pl.multiple_of(head * plan.span + wide, plan.width), plan.landed * plan.width),
        ] = parts[c][...]


def per_device(queries, key_cache, value_cache, key_scale, value_scale, pattern, target):
    groups, shards = lax.axis_size("replica"), lax.axis_size("ctx")
    plan = Plan(queries, key_cache, key_scale, pattern, groups, shards)
    bf16 = jnp.bfloat16
    params = pltpu.CompilerParams(vmem_limit_bytes=32 * 2**20)

    def over_ctx(x, step):
        return lax.ppermute(x, "ctx", [(i, i ^ step) for i in range(shards)])

    def over_pair(x):
        return lax.ppermute(x, "replica", [(i, i ^ 1) for i in range(groups)])

    own, *pieces = pl.pallas_call(
        functools.partial(pack_near, plan),
        in_specs=[VMEM] * 5,
        out_specs=[VMEM] * shards,
        out_shape=[
            jax.ShapeDtypeStruct((plan.cache_rows(c) + plan.near_rows, plan.width), bf16)
            for c in range(shards)
        ],
        scratch_shapes=[pltpu.VMEM((plan.local_blocks, plan.width), jnp.float32)],
        compiler_params=params,
        name="pack_near",
    )(key_scale, value_scale, key_cache, value_cache, queries)
    direct = []
    for c, piece in enumerate(pieces):
        direct.append(over_ctx(piece, c + 1))
    swapped = [over_pair(piece) for piece in direct]
    far = pl.pallas_call(
        functools.partial(pack_far, plan),
        in_specs=[SMEM, VMEM],
        out_specs=VMEM,
        out_shape=jax.ShapeDtypeStruct(
            (groups, shards, plan.chunk, plan.landed * plan.width), bf16
        ),
        compiler_params=params,
        name="pack_far",
    )(target, queries)

    def everywhere(x):
        flat = x.reshape(groups * shards, *x.shape[2:])
        return lax.all_to_all(
            flat, ("replica", "ctx"), split_axis=0, concat_axis=0, tiled=True
        ).reshape(x.shape)

    rows_far = everywhere(far)
    done_near, keys, values, scale = attend(
        plan, False, target, [own, *direct, *swapped, pattern]
    )
    moved = everywhere(done_near)
    done_far = attend(plan, True, target, [rows_far, keys, values, scale, pattern])
    parts = [done_far[0]] + [over_ctx(done_far[c], c) for c in range(1, shards)]
    return pl.pallas_call(
        functools.partial(place_rows, plan),
        in_specs=[SMEM] + [VMEM] * (shards + 1),
        out_specs=VMEM,
        out_shape=jax.ShapeDtypeStruct(queries.shape, bf16),
        scratch_shapes=[pltpu.SMEM((plan.per_group,), jnp.int32)],
        compiler_params=params,
        name="place_rows",
    )(target, moved, *parts)


def solution(mesh):
    return jax.shard_map(
        per_device,
        mesh=mesh,
        in_specs=(
            P("replica", "ctx", None),
            P("ctx", None),
            P("ctx", None),
            P("ctx", None),
            P("ctx", None),
            P(),
            P(),
        ),
        out_specs=P("replica", "ctx", None),
        check_vma=False,
    )
```

time: 484 us -> 94.6 us (0.20)
  waiting for transfers between devices: 189 us -> 33.9 us
  matrix products: 80.3 us -> 0 us
  local copies, waits for them, and re-layouts: 63.9 us -> 4.81 us
  other arithmetic: 57.7 us -> 0 us
  loops' own time: 53.7 us -> 0 us
  starting transfers between devices: 6.47 us -> 31.4 us
  Pallas kernels: 0 us -> 24 us
  blocking collectives: 15.4 us -> 0 us
  between operations: 14 us -> 0.08 us
    unnamed x5 -> x0, waiting for transfers between devices: 104 us -> none
    dot_general x34 -> x0, matrix products: 80.3 us -> none  [the longest x16 49 us: one_item(): jnp.einsum('krbt,btd->rkd', weight, value_head, preferred_element_type=jn...]
    another operation x1 -> x0, loops' own time: 53.7 us -> none  [attend(): lax.map(one_item, jnp.arange(block_count * kv_heads, dtype=jnp.int32))]
    all_to_all x1 -> x2, waiting for transfers between devices: 42.9 us -> 0.01 us  [everywhere(): lax.all_to_all(flat, ('replica', 'ctx'), split_axis=0, concat_axis=0, til...]
    all_gather x1 -> x0, waiting for transfers between devices: 42.8 us -> none  [collect(): return lax.all_gather(blocks, 'ctx', axis=1, tiled=True)]
    ppermute x0 -> x9, waiting for transfers between devices: none -> 33.9 us  [the longest x6 32.3 us: over_ctx(): return lax.ppermute(x, 'ctx', [(i, i ^ step) for i in range(shards)])]
    pallas_call x0 -> x5, Pallas kernels: none -> 24 us  [the longest x2 20.2 us: attend(): pl.pallas_call(functools.partial(attend_body, plan, far, step), in_specs=...]
    dynamic_slice x33 -> x0, local copies, waits for them, and re-layouts: 19.5 us -> none  [the longest x16 9.39 us: one_item(): diag = lax.dynamic_index_in_dim(diagonal, block_slot, 0, keepdims=False)]
  transfers between devices with their start and end apart: 4 -> 11, of which waited for: 4 -> 5; matrix products, arithmetic and copies ran while one was open for 5% -> 0% of each run, Pallas kernels for 0% -> 22%
where the time goes in v1:
time: 94.6 us; the launch traced here: 94.2 us
  waiting for transfers between devices  33.9 us (36%)
  starting transfers between devices  31.4 us (33%)
  Pallas kernels  24 us (25%)
  local copies, waits for them, and re-layouts  4.81 us (5%)
    ppermute x6, waiting for transfers between devices, over_ctx(): return lax.ppermute(x, 'ctx', [(i, i ^ step) for i in range(shards)])  32.3 us
    all_to_all x2, starting transfers between devices, everywhere(): lax.all_to_all(flat, ('replica', 'ctx'), split_axis=0, concat_axis=0, til...  23.7 us
    pallas_call x2, Pallas kernels, attend(): pl.pallas_call(functools.partial(attend_body, plan, far, step), in_specs=...  20.2 us
    ppermute x6, starting transfers between devices, over_ctx(): return lax.ppermute(x, 'ctx', [(i, i ^ step) for i in range(shards)])  7.11 us
    unnamed x24, local copies, waits for them, and re-layouts  4.81 us
    pallas_call x1, Pallas kernels, per_device(): pl.pallas_call(functools.partial(place_rows, plan), in_specs=[SMEM] + [VM...  1.92 us
  transfers between devices with their start and end apart: 11, of which 5 were waited for; matrix products, arithmetic and copies ran while one was open for 0% of the time, Pallas kernels for 22%

profile of v1, /device:TPU:0, one launch (start us, length us, event | category | flops | bytes accessed | tf_op | source)
XLA Modules:
  0.0 94.2 jit_solution(2030859685157749104)
XLA Ops:
  0.0 0.0 copy-start
  0.0 1.2 %copy-done = bf16[4,32,3584]{2,1,0:T(8,128)(2,1)S(1)} copy-done((bf16[4,32,3584]{2,1,0:T(8,128)(2,1)S(1)}, bf16[4,32,3584]{2,1,0:T(8,128)(2,1)}, u32[]{:S(2)}) %copy-start) | copy-done | bytes 917528
  1.2 0.0 copy-start.4
  1.2 0.7 copy-done.4
  1.8 0.0 copy-start.3
  1.8 1.6 %pack_far.1 = bf16[8,4,32,512]{3,2,1,0:T(8,128)(2,1)} custom-call(s32[32]{0:T(128)S(1)} %copy-done.4, bf16[4,32,3584]{2,1,0:T(8,128)(2,1)S(1)} %copy-done), custom_call_target="tpu_custom_call" | custom-call | tf_op jit(solution)/shard_map/pack_far/pallas_call | solution.py:436
  3.4 0.0 copy-start.9
  3.4 0.0 copy-start.1
  3.4 0.0 copy-start.2
  3.4 7.5 %all-to-all-start.1 = ((bf16[32,32,512]{2,1,0:T(8,128)(2,1)}), bf16[32,32,512]{2,1,0:T(8,128)(2,1)}, u32[]{:S(2)}, u32[]{:S(2)}) async-start(bf16[32,32,512]{2,1,0:T(8,128)(2,1)} %bitcast.2), calls=%async_computation.1 | async-start | bytes 2097152 | tf_op jit(solution)/shard_map/all_to_all | solution.py:449
  10.9 0.0 copy-done.9
  10.9 0.0 copy-start.10
  10.9 0.1 copy.8.ks_ref
  11.0 0.6 copy-done.10
  11.6 0.1 copy.9.vs_ref
  11.6 0.0 copy-done.3
  11.6 0.0 copy-done.1
  11.6 0.0 copy-done.2
  11.6 0.0 copy-start.6
  11.7 0.3 pack_near.1
  12.0 1.8 %collective-permute-start = (bf16[1440,128]{1,0:T(8,128)(2,1)S(1)}, bf16[1440,128]{1,0:T(8,128)(2,1)S(1)}, u32[]{:S(2)}, u32[]{:S(2)}) collective-permute-start(bf16[1440,128]{1,0:T(8,128)(2,1)S(1)} %get-tuple-element.18), channel_id=1, source_target_pairs={{0,1},{1,0},{2,3},{3,2},{4,5},{5,4},{6,7},{7,6},{8,9},{9,8},{10,11... | collective-permute-start | bytes 1105928 | tf_op jit(solution)/shard_map/ppermute | solution.py:415
  13.7 1.5 %collective-permute-start.1 = (bf16[1440,128]{1,0:T(8,128)(2,1)S(1)}, bf16[1440,128]{1,0:T(8,128)(2,1)S(1)}, u32[]{:S(2)}, u32[]{:S(2)}) collective-permute-start(bf16[1440,128]{1,0:T(8,128)(2,1)S(1)} %get-tuple-element.19), channel_id=1, source_target_pairs={{0,2},{1,3},{2,0},{3,1},{4,6},{5,7},{6,4},{7,5},{8,10},{9,11},{10,... | collective-permute-start | bytes 1105928 | tf_op jit(solution)/shard_map/ppermute | solution.py:415
  15.2 0.0 copy-start.5
  15.2 0.3 collective-permute-start.2
  15.5 16.7 %collective-permute-done.refs_2_ = bf16[1440,128]{1,0:T(8,128)(2,1)S(1)} collective-permute-done((bf16[1440,128]{1,0:T(8,128)(2,1)S(1)}, bf16[1440,128]{1,0:T(8,128)(2,1)S(1)}, u32[]{:S(2)}, u32[]{:S(2)}) %collective-permute-start) | collective-permute-done | bytes 368672 | tf_op jit(solution)/shard_map/ppermute | solution.py:415
  32.2 0.0 collective-permute-start.3
  32.2 0.0 collective-permute-done.1.refs_3_
  32.2 0.5 collective-permute-start.4
  32.7 9.1 %collective-permute-done.2.refs_4_ = bf16[1440,128]{1,0:T(8,128)(2,1)S(1)} collective-permute-done((bf16[1440,128]{1,0:T(8,128)(2,1)S(1)}, bf16[1440,128]{1,0:T(8,128)(2,1)S(1)}, u32[]{:S(2)}, u32[]{:S(2)}) %collective-permute-start.2) | collective-permute-done | bytes 368672 | tf_op jit(solution)/shard_map/ppermute | solution.py:415
  41.8 0.0 collective-permute-start.5
  41.9 0.0 collective-permute-done.3.refs_5_
  41.9 0.0 collective-permute-done.4.refs_6_
  41.9 1.7 %collective-permute-done.5.refs_7_ = bf16[1440,128]{1,0:T(8,128)(2,1)S(1)} collective-permute-done((bf16[1440,128]{1,0:T(8,128)(2,1)S(1)}, bf16[1440,128]{1,0:T(8,128)(2,1)S(1)}, u32[]{:S(2)}, u32[]{:S(2)}) %collective-permute-start.5) | collective-permute-done | bytes 368672 | tf_op jit(solution)/shard_map/ppermute | solution.py:418
  43.5 0.0 copy-done.6
  43.5 0.0 copy-done.5
  43.5 5.7 %attend_near.1 = (bf16[8,4,32,384]{3,2,1,0:T(8,128)(2,1)}, bf16[4096,128]{1,0:T(8,128)(2,1)S(1)}, bf16[4096,128]{1,0:T(8,128)(2,1)S(1)}, f32[32,128]{1,0:T(8,128)S(1)}) custom-call(s32[32]{0:T(128)S(1)} %copy-done.5, bf16[2464,128]{1,0:T(8,128)(2,1)S(1)} %get-tuple-element.17.refs_1_, bf16[1440,128]{1,0:T(8,128)(2,1)S(1)} %collective-permute-done.refs_2_, ...), custom_call_target="tpu_custom_call" | custom-call | flops 1610612736 | bytes 8388608 | tf_op jit(solution)/shard_map/attend_near/pallas_call | solution.py:354
  49.3 0.0 copy-start.7
  49.3 1.0 %copy-done.7 = bf16[4096,128]{1,0:T(8,128)(2,1)} copy-done((bf16[4096,128]{1,0:T(8,128)(2,1)}, bf16[4096,128]{1,0:T(8,128)(2,1)S(1)}, u32[]{:S(2)}) %copy-start.7) | copy-done | bytes 1048600
  50.3 0.0 all-to-all-done.1
  50.3 16.3 %all-to-all-start = ((bf16[32,32,384]{2,1,0:T(8,128)(2,1)}), bf16[32,32,384]{2,1,0:T(8,128)(2,1)S(1)}, u32[]{:S(2)}, u32[]{:S(2)}) async-start(bf16[32,32,384]{2,1,0:T(8,128)(2,1)} %bitcast), calls=%async_computation | async-start | bytes 1572864 | tf_op jit(solution)/shard_map/all_to_all | solution.py:449
  66.6 0.0 copy-start.8
  66.6 1.2 %copy-done.8 = bf16[4096,128]{1,0:T(8,128)(2,1)S(1)} copy-done((bf16[4096,128]{1,0:T(8,128)(2,1)S(1)}, bf16[4096,128]{1,0:T(8,128)(2,1)}, u32[]{:S(2)}) %copy-start.8) | copy-done | bytes 1048600
  67.8 14.5 %attend_far.1 = (bf16[4,32,512]{2,1,0:T(8,128)(2,1)S(1)}, bf16[4,32,512]{2,1,0:T(8,128)(2,1)S(1)}, bf16[4,32,512]{2,1,0:T(8,128)(2,1)S(1)}, bf16[4,32,512]{2,1,0:T(8,128)(2,1)S(1)}) custom-call(s32[32]{0:T(128)S(1)} %copy-done.5, bf16[8,4,32,512]{3,2,1,0:T(8,128)(2,1)} %bitcast.3.refs_1_, bf16[4096,128]{1,0:T(8,128)(2,1)S(1)} %get-tuple-element.22.refs_2_, ...), custom_call_target="tpu_custom_call" | custom-call | flops 2147483648 | bytes 8388608 | tf_op jit(solution)/shard_map/attend_far/pallas_call | solution.py:354
  82.3 1.8 %collective-permute-start.6 = (bf16[4,32,512]{2,1,0:T(8,128)(2,1)S(1)}, bf16[4,32,512]{2,1,0:T(8,128)(2,1)S(1)}, u32[]{:S(2)}, u32[]{:S(2)}) collective-permute-start(bf16[4,32,512]{2,1,0:T(8,128)(2,1)S(1)} %get-tuple-element.26), channel_id=1, source_target_pairs={{0,1},{1,0},{2,3},{3,2},{4,5},{5,4},{6,7},{7,6},{8,9},{9,8},{10,11... | collective-permute-start | bytes 393224 | tf_op jit(solution)/shard_map/ppermute | solution.py:415
  84.1 1.5 %collective-permute-start.7 = (bf16[4,32,512]{2,1,0:T(8,128)(2,1)S(1)}, bf16[4,32,512]{2,1,0:T(8,128)(2,1)S(1)}, u32[]{:S(2)}, u32[]{:S(2)}) collective-permute-start(bf16[4,32,512]{2,1,0:T(8,128)(2,1)S(1)} %get-tuple-element.27), channel_id=1, source_target_pairs={{0,2},{1,3},{2,0},{3,1},{4,6},{5,7},{6,4},{7,5},{8,10},{9,11},{10,... | collective-permute-start | bytes 393224 | tf_op jit(solution)/shard_map/ppermute | solution.py:415
  85.6 0.3 collective-permute-start.8
  85.8 3.1 %collective-permute-done.6.refs_1_ = bf16[4,32,512]{2,1,0:T(8,128)(2,1)S(1)} collective-permute-done((bf16[4,32,512]{2,1,0:T(8,128)(2,1)S(1)}, bf16[4,32,512]{2,1,0:T(8,128)(2,1)S(1)}, u32[]{:S(2)}, u32[]{:S(2)}) %collective-permute-start.6) | collective-permute-done | bytes 131104 | tf_op jit(solution)/shard_map/ppermute | solution.py:415
  88.9 3.4 %collective-permute-done.7.refs_2_ = bf16[4,32,512]{2,1,0:T(8,128)(2,1)S(1)} collective-permute-done((bf16[4,32,512]{2,1,0:T(8,128)(2,1)S(1)}, bf16[4,32,512]{2,1,0:T(8,128)(2,1)S(1)}, u32[]{:S(2)}, u32[]{:S(2)}) %collective-permute-start.7) | collective-permute-done | bytes 131104 | tf_op jit(solution)/shard_map/ppermute | solution.py:415
  92.3 0.0 collective-permute-done.8.refs_3_
  92.3 0.0 all-to-all-done
  92.3 1.9 %place_rows.1 = bf16[4,32,3584]{2,1,0:T(8,128)(2,1)} custom-call(s32[32]{0:T(128)S(1)} %copy-done.5, bf16[8,4,32,384]{3,2,1,0:T(8,128)(2,1)S(1)} %bitcast.4, bf16[4,32,512]{2,1,0:T(8,128)(2,1)S(1)} %get-tuple-element.25.refs_0_, bf16[4,32,512]{2,1,0:T(8,128)(2,1)S(1)} %collective-permute-done.6.refs_1_, ...), custom_call_target="tpu_custom_call" | custom-call | tf_op jit(solution)/shard_map/place_rows/pallas_call | solution.py:460
Async XLA Ops:
  0.0 1.2 %copy-start = (bf16[4,32,3584]{2,1,0:T(8,128)(2,1)S(1)}, bf16[4,32,3584]{2,1,0:T(8,128)(2,1)}, u32[]{:S(2)}) copy-start(bf16[4,32,3584]{2,1,0:T(8,128)(2,1)} %q_ref.3) | copy-start | bytes 2752516
  1.2 0.7 copy-start.4
  1.8 9.8 %copy-start.3 = (bf16[1024,512]{1,0:T(8,128)(2,1)S(1)}, bf16[1024,512]{1,0:T(8,128)(2,1)}, u32[]{:S(2)}) copy-start(bf16[1024,512]{1,0:T(8,128)(2,1)} %v_ref.1) | copy-start | bytes 3145732
  3.4 7.5 %copy-start.9 = (f32[8,4]{0,1:T(4,128)S(1)}, f32[8,4]{0,1:T(4,128)}, u32[]{:S(2)}) copy-start(f32[8,4]{0,1:T(4,128)} %param.10) | copy-start | bytes 388
  3.4 8.2 %copy-start.1 = (bf16[4,32,3584]{2,1,0:T(8,128)(2,1)S(1)}, bf16[4,32,3584]{2,1,0:T(8,128)(2,1)}, u32[]{:S(2)}) copy-start(bf16[4,32,3584]{2,1,0:T(8,128)(2,1)} %q_ref.3) | copy-start | bytes 2752516
  3.4 8.2 %copy-start.2 = (bf16[1024,512]{1,0:T(8,128)(2,1)S(1)}, bf16[1024,512]{1,0:T(8,128)(2,1)}, u32[]{:S(2)}) copy-start(bf16[1024,512]{1,0:T(8,128)(2,1)} %k_ref.1) | copy-start | bytes 3145732
  3.4 46.9 %all-to-all-start.1 = ((bf16[32,32,512]{2,1,0:T(8,128)(2,1)}), bf16[32,32,512]{2,1,0:T(8,128)(2,1)}, u32[]{:S(2)}, u32[]{:S(2)}) async-start(bf16[32,32,512]{2,1,0:T(8,128)(2,1)} %bitcast.2), calls=%async_computation.1 | async-start | bytes 2097152 | tf_op jit(solution)/shard_map/all_to_all | solution.py:449
  10.9 0.7 copy-start.10
  11.6 31.9 %copy-start.6 = (s32[28,32,32]{2,1,0:T(8,128)S(1)}, s32[28,32,32]{2,1,0:T(8,128)}, u32[]{:S(2)}) copy-start(s32[28,32,32]{2,1,0:T(8,128)} %refs_5_.1) | copy-start | bytes 344068
  12.0 20.3 %collective-permute-start = (bf16[1440,128]{1,0:T(8,128)(2,1)S(1)}, bf16[1440,128]{1,0:T(8,128)(2,1)S(1)}, u32[]{:S(2)}, u32[]{:S(2)}) collective-permute-start(bf16[1440,128]{1,0:T(8,128)(2,1)S(1)} %get-tuple-element.18), channel_id=1, source_target_pairs={{0,1},{1,0},{2,3},{3,2},{4,5},{5,4},{6,7},{7,6},{8,9},{9,8},{10,11... | collective-permute-start | bytes 1105928 | tf_op jit(solution)/shard_map/ppermute | solution.py:415
  13.7 18.5 %collective-permute-start.1 = (bf16[1440,128]{1,0:T(8,128)(2,1)S(1)}, bf16[1440,128]{1,0:T(8,128)(2,1)S(1)}, u32[]{:S(2)}, u32[]{:S(2)}) collective-permute-start(bf16[1440,128]{1,0:T(8,128)(2,1)S(1)} %get-tuple-element.19), channel_id=1, source_target_pairs={{0,2},{1,3},{2,0},{3,1},{4,6},{5,7},{6,4},{7,5},{8,10},{9,11},{10,... | collective-permute-start | bytes 1105928 | tf_op jit(solution)/shard_map/ppermute | solution.py:415
  15.2 28.4 %copy-start.5 = (s32[32]{0:T(128)S(1)}, s32[32]{0:T(128)}, u32[]{:S(2)}) copy-start(s32[32]{0:T(128)} %target.3) | copy-start | bytes 388
  15.2 26.7 %collective-permute-start.2 = (bf16[1440,128]{1,0:T(8,128)(2,1)S(1)}, bf16[1440,128]{1,0:T(8,128)(2,1)S(1)}, u32[]{:S(2)}, u32[]{:S(2)}) collective-permute-start(bf16[1440,128]{1,0:T(8,128)(2,1)S(1)} %get-tuple-element.20), channel_id=1, source_target_pairs={{0,3},{1,2},{2,1},{3,0},{4,7},{5,6},{6,5},{7,4},{8,11},{9,10},{10,... | collective-permute-start | bytes 1105928 | tf_op jit(solution)/shard_map/ppermute | solution.py:415
  32.2 9.6 %collective-permute-start.3 = (bf16[1440,128]{1,0:T(8,128)(2,1)S(1)}, bf16[1440,128]{1,0:T(8,128)(2,1)S(1)}, u32[]{:S(2)}, u32[]{:S(2)}) collective-permute-start(bf16[1440,128]{1,0:T(8,128)(2,1)S(1)} %collective-permute-done.refs_2_), channel_id=1, source_target_pairs={{0,4},{4,0},{8,12},{12,8},{16,20},{20,16},{24,28},{28,24},{1,5},{5... | collective-permute-start | bytes 1105928 | tf_op jit(solution)/shard_map/ppermute | solution.py:418
  32.2 9.6 %collective-permute-start.4 = (bf16[1440,128]{1,0:T(8,128)(2,1)S(1)}, bf16[1440,128]{1,0:T(8,128)(2,1)S(1)}, u32[]{:S(2)}, u32[]{:S(2)}) collective-permute-start(bf16[1440,128]{1,0:T(8,128)(2,1)S(1)} %collective-permute-done.1.refs_3_), channel_id=1, source_target_pairs={{0,4},{4,0},{8,12},{12,8},{16,20},{20,16},{24,28},{28,24},{1,5},{5... | collective-permute-start | bytes 1105928 | tf_op jit(solution)/shard_map/ppermute | solution.py:418
  41.8 1.7 %collective-permute-start.5 = (bf16[1440,128]{1,0:T(8,128)(2,1)S(1)}, bf16[1440,128]{1,0:T(8,128)(2,1)S(1)}, u32[]{:S(2)}, u32[]{:S(2)}) collective-permute-start(bf16[1440,128]{1,0:T(8,128)(2,1)S(1)} %collective-permute-done.2.refs_4_), channel_id=1, source_target_pairs={{0,4},{4,0},{8,12},{12,8},{16,20},{20,16},{24,28},{28,24},{1,5},{5... | collective-permute-start | bytes 1105928 | tf_op jit(solution)/shard_map/ppermute | solution.py:418
  49.3 1.0 %copy-start.7 = (bf16[4096,128]{1,0:T(8,128)(2,1)}, bf16[4096,128]{1,0:T(8,128)(2,1)S(1)}, u32[]{:S(2)}) copy-start(bf16[4096,128]{1,0:T(8,128)(2,1)S(1)} %get-tuple-element.23.refs_3_) | copy-start | bytes 3145732
  50.3 42.0 %all-to-all-start = ((bf16[32,32,384]{2,1,0:T(8,128)(2,1)}), bf16[32,32,384]{2,1,0:T(8,128)(2,1)S(1)}, u32[]{:S(2)}, u32[]{:S(2)}) async-start(bf16[32,32,384]{2,1,0:T(8,128)(2,1)} %bitcast), calls=%async_computation | async-start | bytes 1572864 | tf_op jit(solution)/shard_map/all_to_all | solution.py:449
  66.6 1.2 %copy-start.8 = (bf16[4096,128]{1,0:T(8,128)(2,1)S(1)}, bf16[4096,128]{1,0:T(8,128)(2,1)}, u32[]{:S(2)}) copy-start(bf16[4096,128]{1,0:T(8,128)(2,1)} %copy-done.7) | copy-start | bytes 3145732
  82.3 6.6 %collective-permute-start.6 = (bf16[4,32,512]{2,1,0:T(8,128)(2,1)S(1)}, bf16[4,32,512]{2,1,0:T(8,128)(2,1)S(1)}, u32[]{:S(2)}, u32[]{:S(2)}) collective-permute-start(bf16[4,32,512]{2,1,0:T(8,128)(2,1)S(1)} %get-tuple-element.26), channel_id=1, source_target_pairs={{0,1},{1,0},{2,3},{3,2},{4,5},{5,4},{6,7},{7,6},{8,9},{9,8},{10,11... | collective-permute-start | bytes 393224 | tf_op jit(solution)/shard_map/ppermute | solution.py:415
  84.1 8.2 %collective-permute-start.7 = (bf16[4,32,512]{2,1,0:T(8,128)(2,1)S(1)}, bf16[4,32,512]{2,1,0:T(8,128)(2,1)S(1)}, u32[]{:S(2)}, u32[]{:S(2)}) collective-permute-start(bf16[4,32,512]{2,1,0:T(8,128)(2,1)S(1)} %get-tuple-element.27), channel_id=1, source_target_pairs={{0,2},{1,3},{2,0},{3,1},{4,6},{5,7},{6,4},{7,5},{8,10},{9,11},{10,... | collective-permute-start | bytes 393224 | tf_op jit(solution)/shard_map/ppermute | solution.py:415
  85.6 6.7 %collective-permute-start.8 = (bf16[4,32,512]{2,1,0:T(8,128)(2,1)S(1)}, bf16[4,32,512]{2,1,0:T(8,128)(2,1)S(1)}, u32[]{:S(2)}, u32[]{:S(2)}) collective-permute-start(bf16[4,32,512]{2,1,0:T(8,128)(2,1)S(1)} %get-tuple-element.28), channel_id=1, source_target_pairs={{0,3},{1,2},{2,1},{3,0},{4,7},{5,6},{6,5},{7,4},{8,11},{9,10},{10,... | collective-permute-start | bytes 393224 | tf_op jit(solution)/shard_map/ppermute | solution.py:415
